TPU v7x, 32 devices: a whole 2x2x4 slice. The times are simulated.
32 devices in a mesh: seqs: 2 (over x), rows: 4 (over z), states: 4 (over y, core).
Axes of the slice: x: 2, y: 2, z: 4, core: 2. Of those that a mesh axis runs over, the one named last changes fastest.
Arguments:
- transition: bfloat16 [16384, 16384], P(None, ('rows', 'states'))
- emission: bfloat16 [16384, 10000], P(('rows', 'states'))
- init_probs: float32 [16384], P(('rows', 'states'))
- tokens: int32 [16, 48], P('seqs'), parts along dimension 0
- lengths: int32 [16], P('seqs'), parts along dimension 0
Outputs:
- output 1: float32 [16], P('seqs'), parts along dimension 0
- output 2: float32 [16, 16384], P('seqs', ('rows', 'states')), parts along dimension 0
There are 2 independent parts. A program takes and returns all parts, laid end to end along the dimension named above; an argument that names none is the same for every part.
All inputs are finite; a program needn't handle non-finite values.
Results may differ from a plain program's by a relative error of at most 0.0042.
Values are sent between devices in bfloat16 or wider.
A program may use at most 1 GiB of HBM per device.

v0:
```python
import jax
import jax.numpy as jnp
from jax import lax
from jax.sharding import PartitionSpec as P

STATE_AXES = ('rows', 'states')


def solution(mesh):
    def device_forward(transition_cols, emission_rows, init_probs, tokens, lengths):
        num_steps = tokens.shape[1]
        emit_steps = jnp.transpose(jnp.take(emission_rows, tokens, axis=1), (2, 1, 0))
        alpha_init = init_probs[None, :] * emit_steps[0]
        first_norm = lax.psum(jnp.sum(alpha_init, axis=1), STATE_AXES)
        alpha_init = alpha_init / first_norm[:, None]
        log_init = jnp.log(first_norm)

        def step_body(step_idx, carry):
            alpha_prev, log_acc = carry
            gathered = lax.all_gather(alpha_prev.astype(jnp.bfloat16), STATE_AXES, axis=1, tiled=True)
            predicted = jnp.dot(gathered, transition_cols, preferred_element_type=jnp.float32)
            alpha_new = predicted * emit_steps[step_idx]
            step_norm = lax.psum(jnp.sum(alpha_new, axis=1), STATE_AXES)
            alpha_new = alpha_new / step_norm[:, None]
            alive_rows = step_idx < lengths
            alpha_next = jnp.where(alive_rows[:, None], alpha_new, alpha_prev)
            log_next = log_acc + jnp.where(alive_rows, jnp.log(step_norm), 0.0)
            return alpha_next, log_next

        alpha_last, loglik = lax.fori_loop(1, num_steps, step_body, (alpha_init, log_init))
        return loglik, alpha_last

    return jax.shard_map(
        device_forward,
        mesh=mesh,
        in_specs=(P(None, STATE_AXES), P(STATE_AXES, None), P(STATE_AXES), P('seqs', None), P('seqs')),
        out_specs=(P('seqs'), P('seqs', STATE_AXES)),
        check_vma=False,
    )
```

profile of v0, /device:TPU:0, one launch (start us, length us, event | category | flops | bytes accessed | tf_op | source)
XLA Modules:
  0.0 2988.4 jit_solution(553414282932600652)
XLA Ops:
  15.8 35.0 %psum.21 = f32[8]{0:T(128)S(1)} all-reduce(f32[8]{0:T(128)S(1)} %fusion.1), channel_id=1, replica_groups=mesh['seqs'=2,'rows'=4,'states'=4] {'rows','states'}, use_global_device_ids=true, to_apply=%region_1.2 | all-reduce | flops 8 | bytes 64 | tf_op jit(solution)/shard_map/psum | solution.py:14
  51.5 2936.2 %while.17 = (s32[]{:T(128)}, f32[8,1024]{1,0:T(8,128)S(1)}, f32[8]{0:T(128)S(1)}, s32[8]{0:T(128)}, bf16[16384,1024]{1,0:T(8,128)(2,1)}, /*index=5*/bf16[48,8,10...) while((s32[]{:T(128)}, f32[8,1024]{1,0:T(8,128)S(1)}, f32[8]{0:T(128)S(1)}, s32[8]{0:T(128)}, ...), condition=%wide.region_5.6_spmd, body=%wide.region_2.0_spmd.sunk | while | flops 268484640 | bytes 34292280 | solution.py:30
  144.7 31.6 %psum.23 = f32[8]{0:T(128)S(1)} all-reduce(f32[8]{0:T(128)S(1)} %get-tuple-element.217), channel_id=1, replica_groups=mesh['seqs'=2,'rows'=4,'states'=4] {'rows','states'}, use_global_device_ids=true, to_apply=%region_4.4 | all-reduce | flops 8 | bytes 64 | tf_op jit(solution)/shard_map/while/body/eval_jaxpr/psum | solution.py:23
  207.2 31.6 %psum.23 = f32[8]{0:T(128)S(1)} all-reduce(f32[8]{0:T(128)S(1)} %get-tuple-element.217), channel_id=1, replica_groups=mesh['seqs'=2,'rows'=4,'states'=4] {'rows','states'}, use_global_device_ids=true, to_apply=%region_4.4 | all-reduce | flops 8 | bytes 64 | tf_op jit(solution)/shard_map/while/body/eval_jaxpr/psum | solution.py:23
  269.7 31.6 %psum.23 = f32[8]{0:T(128)S(1)} all-reduce(f32[8]{0:T(128)S(1)} %get-tuple-element.217), channel_id=1, replica_groups=mesh['seqs'=2,'rows'=4,'states'=4] {'rows','states'}, use_global_device_ids=true, to_apply=%region_4.4 | all-reduce | flops 8 | bytes 64 | tf_op jit(solution)/shard_map/while/body/eval_jaxpr/psum | solution.py:23
  332.2 31.6 %psum.23 = f32[8]{0:T(128)S(1)} all-reduce(f32[8]{0:T(128)S(1)} %get-tuple-element.217), channel_id=1, replica_groups=mesh['seqs'=2,'rows'=4,'states'=4] {'rows','states'}, use_global_device_ids=true, to_apply=%region_4.4 | all-reduce | flops 8 | bytes 64 | tf_op jit(solution)/shard_map/while/body/eval_jaxpr/psum | solution.py:23
  394.6 31.6 %psum.23 = f32[8]{0:T(128)S(1)} all-reduce(f32[8]{0:T(128)S(1)} %get-tuple-element.217), channel_id=1, replica_groups=mesh['seqs'=2,'rows'=4,'states'=4] {'rows','states'}, use_global_device_ids=true, to_apply=%region_4.4 | all-reduce | flops 8 | bytes 64 | tf_op jit(solution)/shard_map/while/body/eval_jaxpr/psum | solution.py:23
  457.1 31.6 %psum.23 = f32[8]{0:T(128)S(1)} all-reduce(f32[8]{0:T(128)S(1)} %get-tuple-element.217), channel_id=1, replica_groups=mesh['seqs'=2,'rows'=4,'states'=4] {'rows','states'}, use_global_device_ids=true, to_apply=%region_4.4 | all-reduce | flops 8 | bytes 64 | tf_op jit(solution)/shard_map/while/body/eval_jaxpr/psum | solution.py:23
  519.6 31.6 %psum.23 = f32[8]{0:T(128)S(1)} all-reduce(f32[8]{0:T(128)S(1)} %get-tuple-element.217), channel_id=1, replica_groups=mesh['seqs'=2,'rows'=4,'states'=4] {'rows','states'}, use_global_device_ids=true, to_apply=%region_4.4 | all-reduce | flops 8 | bytes 64 | tf_op jit(solution)/shard_map/while/body/eval_jaxpr/psum | solution.py:23
  582.1 31.6 %psum.23 = f32[8]{0:T(128)S(1)} all-reduce(f32[8]{0:T(128)S(1)} %get-tuple-element.217), channel_id=1, replica_groups=mesh['seqs'=2,'rows'=4,'states'=4] {'rows','states'}, use_global_device_ids=true, to_apply=%region_4.4 | all-reduce | flops 8 | bytes 64 | tf_op jit(solution)/shard_map/while/body/eval_jaxpr/psum | solution.py:23
  644.5 31.6 %psum.23 = f32[8]{0:T(128)S(1)} all-reduce(f32[8]{0:T(128)S(1)} %get-tuple-element.217), channel_id=1, replica_groups=mesh['seqs'=2,'rows'=4,'states'=4] {'rows','states'}, use_global_device_ids=true, to_apply=%region_4.4 | all-reduce | flops 8 | bytes 64 | tf_op jit(solution)/shard_map/while/body/eval_jaxpr/psum | solution.py:23
  707.0 31.6 %psum.23 = f32[8]{0:T(128)S(1)} all-reduce(f32[8]{0:T(128)S(1)} %get-tuple-element.217), channel_id=1, replica_groups=mesh['seqs'=2,'rows'=4,'states'=4] {'rows','states'}, use_global_device_ids=true, to_apply=%region_4.4 | all-reduce | flops 8 | bytes 64 | tf_op jit(solution)/shard_map/while/body/eval_jaxpr/psum | solution.py:23
  769.5 31.6 %psum.23 = f32[8]{0:T(128)S(1)} all-reduce(f32[8]{0:T(128)S(1)} %get-tuple-element.217), channel_id=1, replica_groups=mesh['seqs'=2,'rows'=4,'states'=4] {'rows','states'}, use_global_device_ids=true, to_apply=%region_4.4 | all-reduce | flops 8 | bytes 64 | tf_op jit(solution)/shard_map/while/body/eval_jaxpr/psum | solution.py:23
  831.9 31.6 %psum.23 = f32[8]{0:T(128)S(1)} all-reduce(f32[8]{0:T(128)S(1)} %get-tuple-element.217), channel_id=1, replica_groups=mesh['seqs'=2,'rows'=4,'states'=4] {'rows','states'}, use_global_device_ids=true, to_apply=%region_4.4 | all-reduce | flops 8 | bytes 64 | tf_op jit(solution)/shard_map/while/body/eval_jaxpr/psum | solution.py:23
  894.4 31.6 %psum.23 = f32[8]{0:T(128)S(1)} all-reduce(f32[8]{0:T(128)S(1)} %get-tuple-element.217), channel_id=1, replica_groups=mesh['seqs'=2,'rows'=4,'states'=4] {'rows','states'}, use_global_device_ids=true, to_apply=%region_4.4 | all-reduce | flops 8 | bytes 64 | tf_op jit(solution)/shard_map/while/body/eval_jaxpr/psum | solution.py:23
  956.9 31.6 %psum.23 = f32[8]{0:T(128)S(1)} all-reduce(f32[8]{0:T(128)S(1)} %get-tuple-element.217), channel_id=1, replica_groups=mesh['seqs'=2,'rows'=4,'states'=4] {'rows','states'}, use_global_device_ids=true, to_apply=%region_4.4 | all-reduce | flops 8 | bytes 64 | tf_op jit(solution)/shard_map/while/body/eval_jaxpr/psum | solution.py:23
  1019.4 31.6 %psum.23 = f32[8]{0:T(128)S(1)} all-reduce(f32[8]{0:T(128)S(1)} %get-tuple-element.217), channel_id=1, replica_groups=mesh['seqs'=2,'rows'=4,'states'=4] {'rows','states'}, use_global_device_ids=true, to_apply=%region_4.4 | all-reduce | flops 8 | bytes 64 | tf_op jit(solution)/shard_map/while/body/eval_jaxpr/psum | solution.py:23
  1081.8 31.6 %psum.23 = f32[8]{0:T(128)S(1)} all-reduce(f32[8]{0:T(128)S(1)} %get-tuple-element.217), channel_id=1, replica_groups=mesh['seqs'=2,'rows'=4,'states'=4] {'rows','states'}, use_global_device_ids=true, to_apply=%region_4.4 | all-reduce | flops 8 | bytes 64 | tf_op jit(solution)/shard_map/while/body/eval_jaxpr/psum | solution.py:23
  1144.3 31.6 %psum.23 = f32[8]{0:T(128)S(1)} all-reduce(f32[8]{0:T(128)S(1)} %get-tuple-element.217), channel_id=1, replica_groups=mesh['seqs'=2,'rows'=4,'states'=4] {'rows','states'}, use_global_device_ids=true, to_apply=%region_4.4 | all-reduce | flops 8 | bytes 64 | tf_op jit(solution)/shard_map/while/body/eval_jaxpr/psum | solution.py:23
  1206.8 31.6 %psum.23 = f32[8]{0:T(128)S(1)} all-reduce(f32[8]{0:T(128)S(1)} %get-tuple-element.217), channel_id=1, replica_groups=mesh['seqs'=2,'rows'=4,'states'=4] {'rows','states'}, use_global_device_ids=true, to_apply=%region_4.4 | all-reduce | flops 8 | bytes 64 | tf_op jit(solution)/shard_map/while/body/eval_jaxpr/psum | solution.py:23
  1269.3 31.6 %psum.23 = f32[8]{0:T(128)S(1)} all-reduce(f32[8]{0:T(128)S(1)} %get-tuple-element.217), channel_id=1, replica_groups=mesh['seqs'=2,'rows'=4,'states'=4] {'rows','states'}, use_global_device_ids=true, to_apply=%region_4.4 | all-reduce | flops 8 | bytes 64 | tf_op jit(solution)/shard_map/while/body/eval_jaxpr/psum | solution.py:23
  1331.7 31.6 %psum.23 = f32[8]{0:T(128)S(1)} all-reduce(f32[8]{0:T(128)S(1)} %get-tuple-element.217), channel_id=1, replica_groups=mesh['seqs'=2,'rows'=4,'states'=4] {'rows','states'}, use_global_device_ids=true, to_apply=%region_4.4 | all-reduce | flops 8 | bytes 64 | tf_op jit(solution)/shard_map/while/body/eval_jaxpr/psum | solution.py:23
  1394.2 31.6 %psum.23 = f32[8]{0:T(128)S(1)} all-reduce(f32[8]{0:T(128)S(1)} %get-tuple-element.217), channel_id=1, replica_groups=mesh['seqs'=2,'rows'=4,'states'=4] {'rows','states'}, use_global_device_ids=true, to_apply=%region_4.4 | all-reduce | flops 8 | bytes 64 | tf_op jit(solution)/shard_map/while/body/eval_jaxpr/psum | solution.py:23
  1456.7 31.6 %psum.23 = f32[8]{0:T(128)S(1)} all-reduce(f32[8]{0:T(128)S(1)} %get-tuple-element.217), channel_id=1, replica_groups=mesh['seqs'=2,'rows'=4,'states'=4] {'rows','states'}, use_global_device_ids=true, to_apply=%region_4.4 | all-reduce | flops 8 | bytes 64 | tf_op jit(solution)/shard_map/while/body/eval_jaxpr/psum | solution.py:23
  1519.2 31.6 %psum.23 = f32[8]{0:T(128)S(1)} all-reduce(f32[8]{0:T(128)S(1)} %get-tuple-element.217), channel_id=1, replica_groups=mesh['seqs'=2,'rows'=4,'states'=4] {'rows','states'}, use_global_device_ids=true, to_apply=%region_4.4 | all-reduce | flops 8 | bytes 64 | tf_op jit(solution)/shard_map/while/body/eval_jaxpr/psum | solution.py:23
  1581.6 31.6 %psum.23 = f32[8]{0:T(128)S(1)} all-reduce(f32[8]{0:T(128)S(1)} %get-tuple-element.217), channel_id=1, replica_groups=mesh['seqs'=2,'rows'=4,'states'=4] {'rows','states'}, use_global_device_ids=true, to_apply=%region_4.4 | all-reduce | flops 8 | bytes 64 | tf_op jit(solution)/shard_map/while/body/eval_jaxpr/psum | solution.py:23
  1644.1 31.6 %psum.23 = f32[8]{0:T(128)S(1)} all-reduce(f32[8]{0:T(128)S(1)} %get-tuple-element.217), channel_id=1, replica_groups=mesh['seqs'=2,'rows'=4,'states'=4] {'rows','states'}, use_global_device_ids=true, to_apply=%region_4.4 | all-reduce | flops 8 | bytes 64 | tf_op jit(solution)/shard_map/while/body/eval_jaxpr/psum | solution.py:23
  1706.6 31.6 %psum.23 = f32[8]{0:T(128)S(1)} all-reduce(f32[8]{0:T(128)S(1)} %get-tuple-element.217), channel_id=1, replica_groups=mesh['seqs'=2,'rows'=4,'states'=4] {'rows','states'}, use_global_device_ids=true, to_apply=%region_4.4 | all-reduce | flops 8 | bytes 64 | tf_op jit(solution)/shard_map/while/body/eval_jaxpr/psum | solution.py:23
  1769.1 31.6 %psum.23 = f32[8]{0:T(128)S(1)} all-reduce(f32[8]{0:T(128)S(1)} %get-tuple-element.217), channel_id=1, replica_groups=mesh['seqs'=2,'rows'=4,'states'=4] {'rows','states'}, use_global_device_ids=true, to_apply=%region_4.4 | all-reduce | flops 8 | bytes 64 | tf_op jit(solution)/shard_map/while/body/eval_jaxpr/psum | solution.py:23
  1831.5 31.6 %psum.23 = f32[8]{0:T(128)S(1)} all-reduce(f32[8]{0:T(128)S(1)} %get-tuple-element.217), channel_id=1, replica_groups=mesh['seqs'=2,'rows'=4,'states'=4] {'rows','states'}, use_global_device_ids=true, to_apply=%region_4.4 | all-reduce | flops 8 | bytes 64 | tf_op jit(solution)/shard_map/while/body/eval_jaxpr/psum | solution.py:23
  1894.0 31.6 %psum.23 = f32[8]{0:T(128)S(1)} all-reduce(f32[8]{0:T(128)S(1)} %get-tuple-element.217), channel_id=1, replica_groups=mesh['seqs'=2,'rows'=4,'states'=4] {'rows','states'}, use_global_device_ids=true, to_apply=%region_4.4 | all-reduce | flops 8 | bytes 64 | tf_op jit(solution)/shard_map/while/body/eval_jaxpr/psum | solution.py:23
  1956.5 31.6 %psum.23 = f32[8]{0:T(128)S(1)} all-reduce(f32[8]{0:T(128)S(1)} %get-tuple-element.217), channel_id=1, replica_groups=mesh['seqs'=2,'rows'=4,'states'=4] {'rows','states'}, use_global_device_ids=true, to_apply=%region_4.4 | all-reduce | flops 8 | bytes 64 | tf_op jit(solution)/shard_map/while/body/eval_jaxpr/psum | solution.py:23
  2018.9 31.6 %psum.23 = f32[8]{0:T(128)S(1)} all-reduce(f32[8]{0:T(128)S(1)} %get-tuple-element.217), channel_id=1, replica_groups=mesh['seqs'=2,'rows'=4,'states'=4] {'rows','states'}, use_global_device_ids=true, to_apply=%region_4.4 | all-reduce | flops 8 | bytes 64 | tf_op jit(solution)/shard_map/while/body/eval_jaxpr/psum | solution.py:23
  2081.4 31.6 %psum.23 = f32[8]{0:T(128)S(1)} all-reduce(f32[8]{0:T(128)S(1)} %get-tuple-element.217), channel_id=1, replica_groups=mesh['seqs'=2,'rows'=4,'states'=4] {'rows','states'}, use_global_device_ids=true, to_apply=%region_4.4 | all-reduce | flops 8 | bytes 64 | tf_op jit(solution)/shard_map/while/body/eval_jaxpr/psum | solution.py:23
  2143.9 31.6 %psum.23 = f32[8]{0:T(128)S(1)} all-reduce(f32[8]{0:T(128)S(1)} %get-tuple-element.217), channel_id=1, replica_groups=mesh['seqs'=2,'rows'=4,'states'=4] {'rows','states'}, use_global_device_ids=true, to_apply=%region_4.4 | all-reduce | flops 8 | bytes 64 | tf_op jit(solution)/shard_map/while/body/eval_jaxpr/psum | solution.py:23
  2206.4 31.6 %psum.23 = f32[8]{0:T(128)S(1)} all-reduce(f32[8]{0:T(128)S(1)} %get-tuple-element.217), channel_id=1, replica_groups=mesh['seqs'=2,'rows'=4,'states'=4] {'rows','states'}, use_global_device_ids=true, to_apply=%region_4.4 | all-reduce | flops 8 | bytes 64 | tf_op jit(solution)/shard_map/while/body/eval_jaxpr/psum | solution.py:23
  2268.8 31.6 %psum.23 = f32[8]{0:T(128)S(1)} all-reduce(f32[8]{0:T(128)S(1)} %get-tuple-element.217), channel_id=1, replica_groups=mesh['seqs'=2,'rows'=4,'states'=4] {'rows','states'}, use_global_device_ids=true, to_apply=%region_4.4 | all-reduce | flops 8 | bytes 64 | tf_op jit(solution)/shard_map/while/body/eval_jaxpr/psum | solution.py:23
  2331.3 31.6 %psum.23 = f32[8]{0:T(128)S(1)} all-reduce(f32[8]{0:T(128)S(1)} %get-tuple-element.217), channel_id=1, replica_groups=mesh['seqs'=2,'rows'=4,'states'=4] {'rows','states'}, use_global_device_ids=true, to_apply=%region_4.4 | all-reduce | flops 8 | bytes 64 | tf_op jit(solution)/shard_map/while/body/eval_jaxpr/psum | solution.py:23
  2393.8 31.6 %psum.23 = f32[8]{0:T(128)S(1)} all-reduce(f32[8]{0:T(128)S(1)} %get-tuple-element.217), channel_id=1, replica_groups=mesh['seqs'=2,'rows'=4,'states'=4] {'rows','states'}, use_global_device_ids=true, to_apply=%region_4.4 | all-reduce | flops 8 | bytes 64 | tf_op jit(solution)/shard_map/while/body/eval_jaxpr/psum | solution.py:23
  2456.3 31.6 %psum.23 = f32[8]{0:T(128)S(1)} all-reduce(f32[8]{0:T(128)S(1)} %get-tuple-element.217), channel_id=1, replica_groups=mesh['seqs'=2,'rows'=4,'states'=4] {'rows','states'}, use_global_device_ids=true, to_apply=%region_4.4 | all-reduce | flops 8 | bytes 64 | tf_op jit(solution)/shard_map/while/body/eval_jaxpr/psum | solution.py:23
  2518.7 31.6 %psum.23 = f32[8]{0:T(128)S(1)} all-reduce(f32[8]{0:T(128)S(1)} %get-tuple-element.217), channel_id=1, replica_groups=mesh['seqs'=2,'rows'=4,'states'=4] {'rows','states'}, use_global_device_ids=true, to_apply=%region_4.4 | all-reduce | flops 8 | bytes 64 | tf_op jit(solution)/shard_map/while/body/eval_jaxpr/psum | solution.py:23
  2581.2 31.6 %psum.23 = f32[8]{0:T(128)S(1)} all-reduce(f32[8]{0:T(128)S(1)} %get-tuple-element.217), channel_id=1, replica_groups=mesh['seqs'=2,'rows'=4,'states'=4] {'rows','states'}, use_global_device_ids=true, to_apply=%region_4.4 | all-reduce | flops 8 | bytes 64 | tf_op jit(solution)/shard_map/while/body/eval_jaxpr/psum | solution.py:23
  2643.7 31.6 %psum.23 = f32[8]{0:T(128)S(1)} all-reduce(f32[8]{0:T(128)S(1)} %get-tuple-element.217), channel_id=1, replica_groups=mesh['seqs'=2,'rows'=4,'states'=4] {'rows','states'}, use_global_device_ids=true, to_apply=%region_4.4 | all-reduce | flops 8 | bytes 64 | tf_op jit(solution)/shard_map/while/body/eval_jaxpr/psum | solution.py:23
  2706.2 31.6 %psum.23 = f32[8]{0:T(128)S(1)} all-reduce(f32[8]{0:T(128)S(1)} %get-tuple-element.217), channel_id=1, replica_groups=mesh['seqs'=2,'rows'=4,'states'=4] {'rows','states'}, use_global_device_ids=true, to_apply=%region_4.4 | all-reduce | flops 8 | bytes 64 | tf_op jit(solution)/shard_map/while/body/eval_jaxpr/psum | solution.py:23
  2768.6 31.6 %psum.23 = f32[8]{0:T(128)S(1)} all-reduce(f32[8]{0:T(128)S(1)} %get-tuple-element.217), channel_id=1, replica_groups=mesh['seqs'=2,'rows'=4,'states'=4] {'rows','states'}, use_global_device_ids=true, to_apply=%region_4.4 | all-reduce | flops 8 | bytes 64 | tf_op jit(solution)/shard_map/while/body/eval_jaxpr/psum | solution.py:23
  2831.1 31.6 %psum.23 = f32[8]{0:T(128)S(1)} all-reduce(f32[8]{0:T(128)S(1)} %get-tuple-element.217), channel_id=1, replica_groups=mesh['seqs'=2,'rows'=4,'states'=4] {'rows','states'}, use_global_device_ids=true, to_apply=%region_4.4 | all-reduce | flops 8 | bytes 64 | tf_op jit(solution)/shard_map/while/body/eval_jaxpr/psum | solution.py:23
  2893.6 31.6 %psum.23 = f32[8]{0:T(128)S(1)} all-reduce(f32[8]{0:T(128)S(1)} %get-tuple-element.217), channel_id=1, replica_groups=mesh['seqs'=2,'rows'=4,'states'=4] {'rows','states'}, use_global_device_ids=true, to_apply=%region_4.4 | all-reduce | flops 8 | bytes 64 | tf_op jit(solution)/shard_map/while/body/eval_jaxpr/psum | solution.py:23
  2956.1 31.6 %psum.23 = f32[8]{0:T(128)S(1)} all-reduce(f32[8]{0:T(128)S(1)} %get-tuple-element.217), channel_id=1, replica_groups=mesh['seqs'=2,'rows'=4,'states'=4] {'rows','states'}, use_global_device_ids=true, to_apply=%region_4.4 | all-reduce | flops 8 | bytes 64 | tf_op jit(solution)/shard_map/while/body/eval_jaxpr/psum | solution.py:23
  (344 shorter events, 1498.7 us)
Async XLA Ops:
  51.5 62.4 %copy-start.1 = (s32[8]{0:T(128)S(1)}, s32[8]{0:T(128)}, u32[]{:S(2)}) copy-start(s32[8]{0:T(128)} %get-tuple-element.241) | copy-start | bytes 100 | tf_op jit(solution)/shard_map/while
  113.9 62.4 %copy-start.1 = (s32[8]{0:T(128)S(1)}, s32[8]{0:T(128)}, u32[]{:S(2)}) copy-start(s32[8]{0:T(128)} %get-tuple-element.241) | copy-start | bytes 100 | tf_op jit(solution)/shard_map/while
  176.4 62.4 %copy-start.1 = (s32[8]{0:T(128)S(1)}, s32[8]{0:T(128)}, u32[]{:S(2)}) copy-start(s32[8]{0:T(128)} %get-tuple-element.241) | copy-start | bytes 100 | tf_op jit(solution)/shard_map/while
  238.9 62.4 %copy-start.1 = (s32[8]{0:T(128)S(1)}, s32[8]{0:T(128)}, u32[]{:S(2)}) copy-start(s32[8]{0:T(128)} %get-tuple-element.241) | copy-start | bytes 100 | tf_op jit(solution)/shard_map/while
  301.4 62.4 %copy-start.1 = (s32[8]{0:T(128)S(1)}, s32[8]{0:T(128)}, u32[]{:S(2)}) copy-start(s32[8]{0:T(128)} %get-tuple-element.241) | copy-start | bytes 100 | tf_op jit(solution)/shard_map/while
  363.8 62.4 %copy-start.1 = (s32[8]{0:T(128)S(1)}, s32[8]{0:T(128)}, u32[]{:S(2)}) copy-start(s32[8]{0:T(128)} %get-tuple-element.241) | copy-start | bytes 100 | tf_op jit(solution)/shard_map/while
  426.3 62.4 %copy-start.1 = (s32[8]{0:T(128)S(1)}, s32[8]{0:T(128)}, u32[]{:S(2)}) copy-start(s32[8]{0:T(128)} %get-tuple-element.241) | copy-start | bytes 100 | tf_op jit(solution)/shard_map/while
  488.8 62.4 %copy-start.1 = (s32[8]{0:T(128)S(1)}, s32[8]{0:T(128)}, u32[]{:S(2)}) copy-start(s32[8]{0:T(128)} %get-tuple-element.241) | copy-start | bytes 100 | tf_op jit(solution)/shard_map/while
  551.3 62.4 %copy-start.1 = (s32[8]{0:T(128)S(1)}, s32[8]{0:T(128)}, u32[]{:S(2)}) copy-start(s32[8]{0:T(128)} %get-tuple-element.241) | copy-start | bytes 100 | tf_op jit(solution)/shard_map/while
  613.7 62.4 %copy-start.1 = (s32[8]{0:T(128)S(1)}, s32[8]{0:T(128)}, u32[]{:S(2)}) copy-start(s32[8]{0:T(128)} %get-tuple-element.241) | copy-start | bytes 100 | tf_op jit(solution)/shard_map/while
  676.2 62.4 %copy-start.1 = (s32[8]{0:T(128)S(1)}, s32[8]{0:T(128)}, u32[]{:S(2)}) copy-start(s32[8]{0:T(128)} %get-tuple-element.241) | copy-start | bytes 100 | tf_op jit(solution)/shard_map/while
  738.7 62.4 %copy-start.1 = (s32[8]{0:T(128)S(1)}, s32[8]{0:T(128)}, u32[]{:S(2)}) copy-start(s32[8]{0:T(128)} %get-tuple-element.241) | copy-start | bytes 100 | tf_op jit(solution)/shard_map/while
  801.2 62.4 %copy-start.1 = (s32[8]{0:T(128)S(1)}, s32[8]{0:T(128)}, u32[]{:S(2)}) copy-start(s32[8]{0:T(128)} %get-tuple-element.241) | copy-start | bytes 100 | tf_op jit(solution)/shard_map/while
  863.6 62.4 %copy-start.1 = (s32[8]{0:T(128)S(1)}, s32[8]{0:T(128)}, u32[]{:S(2)}) copy-start(s32[8]{0:T(128)} %get-tuple-element.241) | copy-start | bytes 100 | tf_op jit(solution)/shard_map/while
  926.1 62.4 %copy-start.1 = (s32[8]{0:T(128)S(1)}, s32[8]{0:T(128)}, u32[]{:S(2)}) copy-start(s32[8]{0:T(128)} %get-tuple-element.241) | copy-start | bytes 100 | tf_op jit(solution)/shard_map/while
  988.6 62.4 %copy-start.1 = (s32[8]{0:T(128)S(1)}, s32[8]{0:T(128)}, u32[]{:S(2)}) copy-start(s32[8]{0:T(128)} %get-tuple-element.241) | copy-start | bytes 100 | tf_op jit(solution)/shard_map/while
  1051.1 62.4 %copy-start.1 = (s32[8]{0:T(128)S(1)}, s32[8]{0:T(128)}, u32[]{:S(2)}) copy-start(s32[8]{0:T(128)} %get-tuple-element.241) | copy-start | bytes 100 | tf_op jit(solution)/shard_map/while
  1113.5 62.4 %copy-start.1 = (s32[8]{0:T(128)S(1)}, s32[8]{0:T(128)}, u32[]{:S(2)}) copy-start(s32[8]{0:T(128)} %get-tuple-element.241) | copy-start | bytes 100 | tf_op jit(solution)/shard_map/while
  1176.0 62.4 %copy-start.1 = (s32[8]{0:T(128)S(1)}, s32[8]{0:T(128)}, u32[]{:S(2)}) copy-start(s32[8]{0:T(128)} %get-tuple-element.241) | copy-start | bytes 100 | tf_op jit(solution)/shard_map/while
  1238.5 62.4 %copy-start.1 = (s32[8]{0:T(128)S(1)}, s32[8]{0:T(128)}, u32[]{:S(2)}) copy-start(s32[8]{0:T(128)} %get-tuple-element.241) | copy-start | bytes 100 | tf_op jit(solution)/shard_map/while
  1300.9 62.4 %copy-start.1 = (s32[8]{0:T(128)S(1)}, s32[8]{0:T(128)}, u32[]{:S(2)}) copy-start(s32[8]{0:T(128)} %get-tuple-element.241) | copy-start | bytes 100 | tf_op jit(solution)/shard_map/while
  1363.4 62.4 %copy-start.1 = (s32[8]{0:T(128)S(1)}, s32[8]{0:T(128)}, u32[]{:S(2)}) copy-start(s32[8]{0:T(128)} %get-tuple-element.241) | copy-start | bytes 100 | tf_op jit(solution)/shard_map/while
  1425.9 62.4 %copy-start.1 = (s32[8]{0:T(128)S(1)}, s32[8]{0:T(128)}, u32[]{:S(2)}) copy-start(s32[8]{0:T(128)} %get-tuple-element.241) | copy-start | bytes 100 | tf_op jit(solution)/shard_map/while
  1488.4 62.4 %copy-start.1 = (s32[8]{0:T(128)S(1)}, s32[8]{0:T(128)}, u32[]{:S(2)}) copy-start(s32[8]{0:T(128)} %get-tuple-element.241) | copy-start | bytes 100 | tf_op jit(solution)/shard_map/while
  1550.8 62.4 %copy-start.1 = (s32[8]{0:T(128)S(1)}, s32[8]{0:T(128)}, u32[]{:S(2)}) copy-start(s32[8]{0:T(128)} %get-tuple-element.241) | copy-start | bytes 100 | tf_op jit(solution)/shard_map/while
  1613.3 62.4 %copy-start.1 = (s32[8]{0:T(128)S(1)}, s32[8]{0:T(128)}, u32[]{:S(2)}) copy-start(s32[8]{0:T(128)} %get-tuple-element.241) | copy-start | bytes 100 | tf_op jit(solution)/shard_map/while
  1675.8 62.4 %copy-start.1 = (s32[8]{0:T(128)S(1)}, s32[8]{0:T(128)}, u32[]{:S(2)}) copy-start(s32[8]{0:T(128)} %get-tuple-element.241) | copy-start | bytes 100 | tf_op jit(solution)/shard_map/while
  1738.3 62.4 %copy-start.1 = (s32[8]{0:T(128)S(1)}, s32[8]{0:T(128)}, u32[]{:S(2)}) copy-start(s32[8]{0:T(128)} %get-tuple-element.241) | copy-start | bytes 100 | tf_op jit(solution)/shard_map/while
  1800.7 62.4 %copy-start.1 = (s32[8]{0:T(128)S(1)}, s32[8]{0:T(128)}, u32[]{:S(2)}) copy-start(s32[8]{0:T(128)} %get-tuple-element.241) | copy-start | bytes 100 | tf_op jit(solution)/shard_map/while
  1863.2 62.4 %copy-start.1 = (s32[8]{0:T(128)S(1)}, s32[8]{0:T(128)}, u32[]{:S(2)}) copy-start(s32[8]{0:T(128)} %get-tuple-element.241) | copy-start | bytes 100 | tf_op jit(solution)/shard_map/while
  1925.7 62.4 %copy-start.1 = (s32[8]{0:T(128)S(1)}, s32[8]{0:T(128)}, u32[]{:S(2)}) copy-start(s32[8]{0:T(128)} %get-tuple-element.241) | copy-start | bytes 100 | tf_op jit(solution)/shard_map/while
  1988.2 62.4 %copy-start.1 = (s32[8]{0:T(128)S(1)}, s32[8]{0:T(128)}, u32[]{:S(2)}) copy-start(s32[8]{0:T(128)} %get-tuple-element.241) | copy-start | bytes 100 | tf_op jit(solution)/shard_map/while
  2050.6 62.4 %copy-start.1 = (s32[8]{0:T(128)S(1)}, s32[8]{0:T(128)}, u32[]{:S(2)}) copy-start(s32[8]{0:T(128)} %get-tuple-element.241) | copy-start | bytes 100 | tf_op jit(solution)/shard_map/while
  2113.1 62.4 %copy-start.1 = (s32[8]{0:T(128)S(1)}, s32[8]{0:T(128)}, u32[]{:S(2)}) copy-start(s32[8]{0:T(128)} %get-tuple-element.241) | copy-start | bytes 100 | tf_op jit(solution)/shard_map/while
  2175.6 62.4 %copy-start.1 = (s32[8]{0:T(128)S(1)}, s32[8]{0:T(128)}, u32[]{:S(2)}) copy-start(s32[8]{0:T(128)} %get-tuple-element.241) | copy-start | bytes 100 | tf_op jit(solution)/shard_map/while
  2238.1 62.4 %copy-start.1 = (s32[8]{0:T(128)S(1)}, s32[8]{0:T(128)}, u32[]{:S(2)}) copy-start(s32[8]{0:T(128)} %get-tuple-element.241) | copy-start | bytes 100 | tf_op jit(solution)/shard_map/while
  2300.5 62.4 %copy-start.1 = (s32[8]{0:T(128)S(1)}, s32[8]{0:T(128)}, u32[]{:S(2)}) copy-start(s32[8]{0:T(128)} %get-tuple-element.241) | copy-start | bytes 100 | tf_op jit(solution)/shard_map/while
  2363.0 62.4 %copy-start.1 = (s32[8]{0:T(128)S(1)}, s32[8]{0:T(128)}, u32[]{:S(2)}) copy-start(s32[8]{0:T(128)} %get-tuple-element.241) | copy-start | bytes 100 | tf_op jit(solution)/shard_map/while
  2425.5 62.4 %copy-start.1 = (s32[8]{0:T(128)S(1)}, s32[8]{0:T(128)}, u32[]{:S(2)}) copy-start(s32[8]{0:T(128)} %get-tuple-element.241) | copy-start | bytes 100 | tf_op jit(solution)/shard_map/while
  2487.9 62.4 %copy-start.1 = (s32[8]{0:T(128)S(1)}, s32[8]{0:T(128)}, u32[]{:S(2)}) copy-start(s32[8]{0:T(128)} %get-tuple-element.241) | copy-start | bytes 100 | tf_op jit(solution)/shard_map/while
  2550.4 62.4 %copy-start.1 = (s32[8]{0:T(128)S(1)}, s32[8]{0:T(128)}, u32[]{:S(2)}) copy-start(s32[8]{0:T(128)} %get-tuple-element.241) | copy-start | bytes 100 | tf_op jit(solution)/shard_map/while
  2612.9 62.4 %copy-start.1 = (s32[8]{0:T(128)S(1)}, s32[8]{0:T(128)}, u32[]{:S(2)}) copy-start(s32[8]{0:T(128)} %get-tuple-element.241) | copy-start | bytes 100 | tf_op jit(solution)/shard_map/while
  2675.4 62.4 %copy-start.1 = (s32[8]{0:T(128)S(1)}, s32[8]{0:T(128)}, u32[]{:S(2)}) copy-start(s32[8]{0:T(128)} %get-tuple-element.241) | copy-start | bytes 100 | tf_op jit(solution)/shard_map/while
  2737.8 62.4 %copy-start.1 = (s32[8]{0:T(128)S(1)}, s32[8]{0:T(128)}, u32[]{:S(2)}) copy-start(s32[8]{0:T(128)} %get-tuple-element.241) | copy-start | bytes 100 | tf_op jit(solution)/shard_map/while
  2800.3 62.4 %copy-start.1 = (s32[8]{0:T(128)S(1)}, s32[8]{0:T(128)}, u32[]{:S(2)}) copy-start(s32[8]{0:T(128)} %get-tuple-element.241) | copy-start | bytes 100 | tf_op jit(solution)/shard_map/while
  2862.8 62.4 %copy-start.1 = (s32[8]{0:T(128)S(1)}, s32[8]{0:T(128)}, u32[]{:S(2)}) copy-start(s32[8]{0:T(128)} %get-tuple-element.241) | copy-start | bytes 100 | tf_op jit(solution)/shard_map/while
  2925.3 62.4 %copy-start.1 = (s32[8]{0:T(128)S(1)}, s32[8]{0:T(128)}, u32[]{:S(2)}) copy-start(s32[8]{0:T(128)} %get-tuple-element.241) | copy-start | bytes 100 | tf_op jit(solution)/shard_map/while
  2987.7 0.6 copy-start.2
  (1 other events, 0.6 us)
where the time goes:
time: 2990 us
  blocking collectives  2360 us (79%)
  matrix products  607 us (20%)
    psum x47, blocking collectives, step_body(): step_norm = lax.psum(jnp.sum(alpha_new, axis=1), STATE_AXES)  1480 us
    all_gather x47, blocking collectives, step_body(): lax.all_gather(alpha_prev.astype(jnp.bfloat16), STATE_AXES, axis=1, tiled...  839 us
    dot_general x47, matrix products, step_body(): jnp.dot(gathered, transition_cols, preferred_element_type=jnp.float32)  607 us

commit v1 on v0

v1 whole, which is shorter than its diff:
```python
import functools
import jax
import jax.numpy as jnp
from jax import lax
from jax.experimental import pallas as pl
from jax.experimental.pallas import tpu as pltpu
from jax.sharding import PartitionSpec as P

STATE_AXES = ('rows', 'states')
ROWS, COLS = 4, 4
NUM_DEV = ROWS * COLS


def forward_kernel(trans_hbm, emit_ref, init_ref, len_ref, ll_ref, alpha_ref,
                   trans, gath, sums, load_sem, send_sem, csend_sem, recv_sem, crecv_sem):
    num_steps, batch, width = emit_ref.shape
    row = lax.axis_index('rows')
    col = lax.axis_index('states')

    def dev(r, s):
        return {'rows': r, 'states': s}

    r1 = row + 1 - 2 * lax.rem(row, 2)
    r2 = lax.rem(row + 2, 4)
    r3 = 3 - row
    sib = col + 1 - 2 * lax.rem(col, 2)
    opp = lax.rem(col + 2, 4)
    osib = opp + 1 - 2 * lax.rem(opp, 2)

    def blk(r, s):
        return r * COLS + s

    me = blk(row, col)

    load = pltpu.make_async_copy(trans_hbm, trans, load_sem)
    load.start()

    barrier = pltpu.get_barrier_semaphore()
    for d in range(1, NUM_DEV):
        peer = lax.rem(me + d, NUM_DEV)
        pl.semaphore_signal(barrier, inc=1, device_id=dev(peer // COLS, lax.rem(peer, COLS)),
                            device_id_type=pl.DeviceIdType.MESH)
    pl.semaphore_wait(barrier, NUM_DEV - 1)

    lane = lax.broadcasted_iota(jnp.int32, (batch, 128), 1)
    sub = lax.broadcasted_iota(jnp.int32, (batch, 128), 0)
    diag = lane == sub

    def send(p, k, slot, r, s):
        return pltpu.make_async_remote_copy(
            src_ref=gath.at[p, k], dst_ref=gath.at[p, k],
            send_sem=send_sem.at[slot], recv_sem=recv_sem.at[p, k],
            device_id=dev(r, s), device_id_type=pl.DeviceIdType.MESH)

    def csend(p, k, slot, r, s):
        return pltpu.make_async_remote_copy(
            src_ref=sums.at[p, k], dst_ref=sums.at[p, k],
            send_sem=csend_sem.at[slot], recv_sem=crecv_sem.at[p, k],
            device_id=dev(r, s), device_id_type=pl.DeviceIdType.MESH)

    def send_sums(p, a):
        total = jnp.sum(a, axis=1, keepdims=True)
        flat = jnp.sum(jnp.where(diag, total, 0.0), axis=0, keepdims=True)
        sums[p, me] = flat
        out = []
        for r in (r3, r2, r1, row):
            for s in (osib, opp, sib, col):
                if r is row and s is col:
                    continue
                c = csend(p, me, len(out), r, s)
                c.start()
                out.append(c)
        return out

    def wait_sums(p):
        for r in (row, r1, r2, r3):
            for s in (sib, opp, osib, col):
                if r is row and s is col:
                    continue
                csend(p, blk(r, s), 0, r, s).wait_recv()
        flat = jnp.sum(sums[p], axis=0)
        return jnp.sum(jnp.where(diag, jnp.broadcast_to(flat, (batch, 128)), 0.0), axis=1, keepdims=True)

    def update(t, a, c):
        alive = t < len_ref[...]
        alpha_ref[...] = jnp.where(alive[:, :1], a / c, alpha_ref[...])
        ll_ref[...] = ll_ref[...] + jnp.where(alive, jnp.log(jnp.broadcast_to(c, (batch, 128))), 0.0)

    ll_ref[...] = jnp.zeros_like(ll_ref)
    alpha_ref[...] = jnp.zeros_like(alpha_ref)

    def body(t, a):
        p = lax.rem(t, 2)
        gath[p, me] = a
        started = send_sums(p, a)
        slot = [0]

        def go(k, r, s):
            c = send(p, k, slot[0], r, s)
            slot[0] += 1
            c.start()
            started.append(c)

        def got(r, s):
            send(p, blk(r, s), 0, r, s).wait_recv()

        go(me, r3, col)
        go(me, r2, col)
        go(me, r1, col)
        go(me, row, opp)
        go(me, row, sib)
        got(row, opp)
        go(blk(row, opp), row, sib)
        for r in (r1, r2, r3):
            got(r, col)
            go(blk(r, col), row, opp)
            go(blk(r, col), row, sib)
        c = wait_sums(p)
        update(t, a, c)

        def part(r, s):
            k = blk(r, s)
            lhs = (gath[p, k] / c).astype(jnp.bfloat16)
            rhs = trans[pl.ds(pl.multiple_of(k * width, width), width), :]
            return jnp.dot(lhs, rhs, preferred_element_type=jnp.float32)

        u = part(row, col)
        u += part(row, opp)
        got(row, sib)
        u += part(row, sib)
        got(r1, opp)
        go(blk(r1, opp), row, sib)
        u += part(r1, col)
        u += part(r2, col)
        u += part(r3, col)
        got(r2, opp)
        go(blk(r2, opp), row, sib)
        u += part(r1, opp)
        got(r1, sib)
        got(row, osib)
        u += part(r1, sib)
        u += part(row, osib)
        got(r3, opp)
        go(blk(r3, opp), row, sib)
        got(r2, sib)
        got(r3, sib)
        u += part(r2, opp)
        u += part(r3, opp)
        u += part(r2, sib)
        u += part(r3, sib)
        got(r1, osib)
        u += part(r1, osib)
        got(r2, osib)
        u += part(r2, osib)
        got(r3, osib)
        u += part(r3, osib)
        for s in started:
            s.wait_send()
        return u * emit_ref[t + 1]

    first = init_ref[...] * emit_ref[0]
    load.wait()
    last = lax.fori_loop(0, num_steps - 1, body, first)
    p = (num_steps - 1) % 2
    started = send_sums(p, last)
    c = wait_sums(p)
    update(num_steps - 1, last, c)
    for s in started:
        s.wait_send()


def solution(mesh):
    def device_forward(transition_cols, emission_rows, init_probs, tokens, lengths):
        batch, num_steps = tokens.shape
        width, vocab = emission_rows.shape
        states = transition_cols.shape[0]
        picks = tokens.T.reshape(-1)
        onehot = (picks[:, None] == lax.broadcasted_iota(jnp.int32, (1, vocab), 1)).astype(jnp.bfloat16)
        emit = lax.dot_general(onehot, emission_rows, (((1,), (1,)), ((), ())),
                               preferred_element_type=jnp.float32)
        emit = emit.reshape(num_steps, batch, width)
        len_b = jnp.broadcast_to(lengths[:, None], (batch, 128))

        vmem = pl.BlockSpec(memory_space=pltpu.VMEM)
        ll, alpha = pl.pallas_call(
            forward_kernel,
            out_shape=(jax.ShapeDtypeStruct((batch, 128), jnp.float32),
                       jax.ShapeDtypeStruct((batch, width), jnp.float32)),
            in_specs=[pl.BlockSpec(memory_space=pl.ANY), vmem, vmem, vmem],
            out_specs=(vmem, vmem),
            scratch_shapes=[
                pltpu.VMEM((states, width), jnp.bfloat16),
                pltpu.VMEM((2, NUM_DEV, batch, width), jnp.float32),
                pltpu.VMEM((2, NUM_DEV, 1, 128), jnp.float32),
                pltpu.SemaphoreType.DMA,
                pltpu.SemaphoreType.DMA((16,)),
                pltpu.SemaphoreType.DMA((NUM_DEV,)),
                pltpu.SemaphoreType.DMA((2, NUM_DEV)),
                pltpu.SemaphoreType.DMA((2, NUM_DEV)),
            ],
            compiler_params=pltpu.CompilerParams(
                collective_id=0, has_side_effects=True, vmem_limit_bytes=56 * 1024 * 1024),
        )(transition_cols, emit, init_probs[None, :], len_b)
        return ll[:, 0], alpha

    return jax.shard_map(
        device_forward,
        mesh=mesh,
        in_specs=(P(None, STATE_AXES), P(STATE_AXES, None), P(STATE_AXES), P('seqs', None), P('seqs')),
        out_specs=(P('seqs'), P('seqs', STATE_AXES)),
        check_vma=False,
    )
```

time: 2990 us -> 548 us (0.18)
  blocking collectives: 2360 us -> 0 us
  matrix products: 607 us -> 12.9 us
  Pallas kernels: 0 us -> 529 us
    psum x48 -> x0, blocking collectives: 1520 us -> none  [the longest x47 1480 us: step_body(): step_norm = lax.psum(jnp.sum(alpha_new, axis=1), STATE_AXES)]
    all_gather x47 -> x0, blocking collectives: 839 us -> none  [step_body(): lax.all_gather(alpha_prev.astype(jnp.bfloat16), STATE_AXES, axis=1, tiled...]
    dot_general x47 -> x1, matrix products: 607 us -> 12.9 us  [device_forward(): lax.dot_general(onehot, emission_rows, (((1,), (1,)), ((), ())), preferre...]
    pallas_call x0 -> x1, Pallas kernels: none -> 529 us  [device_forward(): pl.pallas_call(forward_kernel, out_shape=(jax.ShapeDtypeStruct((batch, 12...]
where the time goes in v1:
time: 548 us; the launch traced here: 547 us
  Pallas kernels  529 us (97%)
  matrix products  12.9 us (2%)
    pallas_call x1, Pallas kernels, device_forward(): pl.pallas_call(forward_kernel, out_shape=(jax.ShapeDtypeStruct((batch, 12...  529 us
    dot_general x1, matrix products, device_forward(): lax.dot_general(onehot, emission_rows, (((1,), (1,)), ((), ())), preferre...  12.9 us

profile of v1, /device:TPU:0, one launch (start us, length us, event | category | flops | bytes accessed | tf_op | source)
XLA Modules:
  0.0 547.3 jit_solution(15690946774985501681)
XLA Ops:
  0.6 1.3 broadcast_in_dim.10.len_ref
  1.9 0.8 copy.7
  2.7 0.1 eq.15
  2.8 12.9 %fusion.2.emit_ref = f32[48,8,1024]{2,1,0:T(8,128)} fusion(bf16[1024,10000]{0,1:T(8,128)(2,1)} %param.6, s32[384]{0:T(512)S(1)} %eq.15), kind=kOutput, calls=%fused_computation.3 | convolution fusion | flops 7868160000 | bytes 22054400 | tf_op jit(solution)/shard_map/dot_general | solution.py:179
  15.7 528.9 %shard_map.68 = (f32[8,128]{1,0:T(8,128)}, f32[8,1024]{1,0:T(8,128)}) custom-call(bf16[16384,1024]{1,0:T(8,128)(2,1)} %trans_hbm.1, f32[48,8,1024]{2,1,0:T(8,128)} %fusion.2.emit_ref, f32[1,1024]{1,0:T(1,128)} %bitcast.5, s32[8,128]{1,0:T(8,128)} %broadcast_in_dim.10.len_ref), custom_call_target="tpu_custom_call" | custom-call | tf_op jit(solution)/shard_map/pallas_call | solution.py:185
  544.6 1.3 slice_reduce_fusion
  545.9 1.4 copy.9
